TPU v7x, 8 devices: a whole 2x2x1 slice. The times are simulated.
8 devices in a mesh: dp: 1 (over z), ep2: 2 (over y), ep: 4 (over x, core).
Axes of the slice: x: 2, y: 2, z: 1, core: 2. Of those that a mesh axis runs over, the one named last changes fastest.
Arguments:
- x_tok: bfloat16 [16384, 768], P(('dp', 'ep2', 'ep'))
- expert_ids: int32 [16384, 1], P(('dp', 'ep2', 'ep'))
- gate_w: float32 [16384, 1], P(('dp', 'ep2', 'ep'))
- w_in: bfloat16 [128, 768, 3072], P(('ep2', 'ep'))
- w_out: bfloat16 [128, 3072, 768], P(('ep2', 'ep'))
Outputs:
- output: bfloat16 [16384, 768], P(('dp', 'ep2', 'ep'))
All inputs are finite; a program needn't handle non-finite values.
Results may differ from a plain program's by a relative error of at most 0.001.
Values are sent between devices in bfloat16 or wider.
A program may use at most 1 GiB of HBM per device.

v0:
```python
import functools

import jax
import jax.numpy as jnp
from jax import lax
from jax.experimental import pallas as pl
from jax.experimental.pallas import tpu as pltpu
from jax.sharding import PartitionSpec as P

MESH = pl.DeviceIdType.MESH
F32 = jnp.float32
BF16 = jnp.bfloat16
GROUP = 8
EXPERTS = 128
E_LOC = EXPERTS // GROUP
SPAN = 512
Z = 32
ROWS = GROUP * Z
PER = 2
SETS = E_LOC // PER
FTILE = 1536
TTILE = 256


def pick(values, i):
    out = values[0]
    for m in range(1, len(values)):
        out = out + (values[m] - values[m - 1]) * ((i + 16 - m) // 16)
    return out


class Plan:
    def __init__(self, lo, hi, slots, batches):
        self.lo, self.hi, self.slots = lo, hi, slots
        self.chunks = hi[-1]
        self.batches = batches
        assert sum(batches) == self.chunks
        self.hi_before = (0,) + hi[:-1]
        self.lo_next = lo[1:] + (self.chunks,)
        self.pairs = tuple((h - l + 1) // 2 for l, h in zip(lo, hi))
        first = [min(m for m in range(SETS) if hi[m] > c) for c in range(self.chunks)]
        after = [max(m for m in range(SETS) if lo[m] <= c) + 1 for c in range(self.chunks)]
        self.wide = max(b - a for a, b in zip(first, after))
        self.first = tuple(min(m, SETS - self.wide) for m in first)
        assert all(h >= 2 * p for h, p in zip(hi, self.pairs))


FAST = Plan((0, 1, 2, 3, 4, 6, 7, 9), (2, 4, 6, 7, 8, 9, 10, 11), 5, (4, 4, 2, 1))
SAFE = Plan((0,) * 8, (2, 4, 6, 8, 10, 12, 14, 16), 3, (4, 4, 4, 4))


def position():
    ep = lax.axis_index('ep')
    return lax.axis_index('ep2'), ep // 2, ep % 2


def partner(where, k):
    y, x, c = where
    py = (y + k // 4) % 2
    px = (x + (k // 2) % 2) % 2
    pc = (c + k % 2) % 2
    return py * 4 + px * 2 + pc, {'ep2': py, 'ep': px * 2 + pc}


def iota(shape, dim):
    return lax.broadcasted_iota(jnp.int32, shape, dim)


def hot(mask):
    return jnp.where(mask, 1.0, 0.0).astype(BF16)


def dot(a, b):
    return jnp.dot(a, b, preferred_element_type=F32)


def moe_kernel(plan, capacity, ids_ref, x_hbm, w_in, w_out, got, flag_ref,
               xv, send, recv, rrecv, bbuf, obuf, acc, wi, wo, xbuf, cbuf, qrow, qcol, dlc, drc,
               x_sem, n_send, n_recv, s_send, s_recv, r_send, r_recv, wi_sem, wo_sem):
    nc, ns = plan.chunks, plan.slots
    n_tok, d_model = xv.shape
    per_e = w_in.shape[2] // FTILE
    slots = PER * capacity
    where = position()
    me = partner(where, 0)[0]

    def w_copies(i, slot):
        e, f = i // per_e, i % per_e
        cols = pl.ds(pl.multiple_of(f * FTILE, FTILE), FTILE)
        return (pltpu.make_async_copy(w_in.at[e, :, cols], wi.at[slot], wi_sem.at[slot]),
                pltpu.make_async_copy(w_out.at[e, cols, :], wo.at[slot], wo_sem.at[slot]))

    def remote(src, dst, sent, received, k):
        return pltpu.make_async_remote_copy(src_ref=src, dst_ref=dst, send_sem=sent, recv_sem=received,
                                            device_id=partner(where, k)[1], device_id_type=MESH)

    def count_copy(k):
        return remote(xbuf.at[k], cbuf.at[k], n_send.at[k], n_recv.at[k], k)

    def out_copy(c, k):
        return remote(send.at[c, k], recv.at[c, k], s_send.at[c, k], s_recv.at[c, k], k)

    def back_copy(c, k):
        return remote(send.at[c, k], rrecv.at[c, k], r_send.at[c, k], r_recv.at[c, k], k)

    barrier = pltpu.get_barrier_semaphore()
    for k in range(1, GROUP):
        pl.semaphore_signal(barrier, inc=1, device_id=partner(where, k)[1], device_id_type=MESH)
    x_copy = pltpu.make_async_copy(x_hbm, xv, x_sem)
    x_copy.start()

    obuf[...] = jnp.zeros_like(obuf)

    row, col = iota((EXPERTS, EXPERTS), 0), iota((EXPERTS, EXPERTS), 1)
    same = (row // E_LOC) == (col // E_LOC)
    in_row, in_col = (row % E_LOC) // PER, (col % E_LOC) // PER
    inner = hot(same & (in_row == in_col) & (col < row))
    sums = [hot(same & (in_col == g)) for g in range(SETS)]

    def starts(counts):
        counts = counts.astype(BF16)
        base = jnp.zeros((EXPERTS, EXPERTS), F32)
        mine, over = base, base
        for g in range(SETS):
            if g:
                base = jnp.maximum(base, float(plan.lo[g] * Z))
            mine = jnp.where(in_row == g, base, mine)
            base = base + dot(sums[g], counts)
            over = jnp.maximum(over, base - float(plan.hi[g] * Z))
        return mine + dot(inner, counts), over

    chosen = hot(iota((EXPERTS, n_tok), 0) == ids_ref[...])
    counts = dot(chosen, jnp.ones((n_tok, 128), BF16))
    start, over = starts(counts)
    to_k = jnp.bitwise_xor(row // E_LOC, me).astype(F32)
    code0 = to_k * float(SPAN) + start

    upper = hot((iota((TTILE, TTILE + 128), 0) < iota((TTILE, TTILE + 128), 1)) | (iota((TTILE, TTILE + 128), 1) >= TTILE))
    base = code0
    for b in range(n_tok // TTILE):
        part = chosen[:, b * TTILE:(b + 1) * TTILE]
        rank = dot(part, upper)
        full = jnp.concatenate([rank[:, i * 128:(i + 1) * 128] + base for i in range(TTILE // 128)], axis=1)
        code = jnp.sum(part.astype(F32) * full, axis=0, keepdims=True)
        qrow[:, b * TTILE:(b + 1) * TTILE] = jnp.broadcast_to(code, (8, TTILE))
        base = base + rank[:, TTILE:]

    worst = jnp.broadcast_to(jnp.max(over, keepdims=True), (8, 128))
    acc[0:EXPERTS, 0:128] = counts
    for k in range(GROUP):
        at = pl.ds(pl.multiple_of(partner(where, k)[0] * E_LOC, E_LOC), E_LOC)
        xbuf[k, 0:E_LOC, :] = acc[at, 0:128]
        xbuf[k, E_LOC:E_LOC + 8, :] = worst
    cbuf[0] = xbuf[0]

    def targets(shape, dim):
        i = iota(shape, dim)
        k = jnp.zeros(shape, jnp.int32)
        c = k
        for m in range(1, -(-shape[dim] // ROWS)):
            c = c + jnp.where(i >= m * ROWS, 1, 0)
        i = i - c * ROWS
        for m in range(1, GROUP):
            k = k + jnp.where(i >= m * Z, 1, 0)
        return (i + k * (SPAN - Z) + c * Z).astype(F32)

    tcol = targets((ROWS, 1), 0)
    trow = targets((1, 4 * ROWS), 1)

    pl.semaphore_wait(barrier, GROUP - 1)
    for k in range(1, GROUP):
        count_copy(k).start()
    x_copy.wait()
    for i in range(ns):
        for copy in w_copies(i, i):
            copy.start()

    @pl.loop(0, nc)
    def _(c):
        mask = (tcol + (c * Z).astype(F32)) == qrow[0:1, :]
        send[c] = dot(hot(mask), xv[...]).astype(BF16).reshape(GROUP, Z, d_model)
        for k in range(GROUP - 1, 0, -1):
            out_copy(c, k).start()
        recv[c, 0] = send[c, 0]

    for b in range(n_tok // TTILE):
        piece = jnp.broadcast_to(qrow[0:1, b * TTILE:(b + 1) * TTILE], (128, TTILE))
        qcol[b * TTILE:(b + 1) * TTILE, :] = jnp.transpose(piece)
    for k in range(1, GROUP):
        count_copy(k).wait_recv()
    flag_ref[0, 0] = jnp.max(cbuf[:, E_LOC:E_LOC + 8, :])
    got_counts = cbuf[:, 0:E_LOC, :].reshape(EXPERTS, 128)
    start, _ = starts(got_counts)
    earlier = hot(((row % E_LOC) == (col % E_LOC)) & (jnp.bitwise_xor(col // E_LOC, me) < jnp.bitwise_xor(row // E_LOC, me)))
    ahead = dot(earlier, got_counts.astype(BF16))
    first = ((row // E_LOC) * SPAN).astype(F32) + start
    kept = jnp.minimum(got_counts, jnp.maximum(capacity - ahead, 0.0))
    last = first + kept
    shift = ((row % E_LOC) * capacity + 1).astype(F32) + ahead - first
    first, last, shift = first[:, 0:1], last[:, 0:1], shift[:, 0:1]
    for c in range(nc):
        at = trow[:, 0:ROWS] + float(c * Z)
        slot = jnp.sum(jnp.where((at >= first) & (at < last), at + shift, 0.0), axis=0, keepdims=True) - 1.0
        dlc[c] = jnp.broadcast_to(slot, (8, ROWS))
        drc[c] = jnp.transpose(jnp.broadcast_to(slot, (128, ROWS)))

    slot_col = iota((slots, 1), 0).astype(F32)
    slot_row = iota((1, plan.wide * slots), 1).astype(F32)

    @pl.loop(0, SETS)
    def _(g):
        @pl.loop(pick(plan.hi_before, g), pick(plan.hi, g))
        def _(c):
            for k in range(1, GROUP):
                out_copy(c, k).wait_recv()

        acc[...] = jnp.zeros_like(acc)

        @pl.loop(0, pick(plan.pairs, g))
        def _(p):
            c = pick(plan.hi, g) - 2 * p - 2
            slot = jnp.concatenate([dlc[c, 0:1, :], dlc[c + 1, 0:1, :]], axis=1)
            mask = (slot_col + (g * slots).astype(F32)) == slot
            acc[...] += dot(hot(mask), recv[pl.ds(c, 2)].reshape(2 * ROWS, d_model))

        bbuf[...] = acc[...].astype(BF16)

        @pl.loop(0, PER)
        def _(j):
            at = pl.ds(pl.multiple_of(j * capacity, capacity), capacity)
            first_i = (g * PER + j) * per_e
            total = None
            for f in range(per_e):
                i = first_i + f
                slot = i % ns
                for copy in w_copies(i, slot):
                    copy.wait()
                v = dot(bbuf[at, :], wi[slot])
                u = v * (0.7978845608028654 + (0.7978845608028654 * 0.044715) * (v * v))
                half = 0.5 * v
                part = dot((half + half * jnp.tanh(u)).astype(BF16), wo[slot])
                total = part if total is None else total + part

                @pl.when(i + ns < E_LOC * per_e)
                def _():
                    for copy in w_copies(i + ns, slot):
                        copy.start()
            obuf[g, at, :] = total.astype(BF16)

        @pl.loop(pick(plan.lo, g), pick(plan.lo_next, g))
        def _(c):
            m = pick(plan.first, c)
            mask = drc[c, :, 0:1] == (slot_row + (m * slots).astype(F32))
            packed = dot(hot(mask), obuf[pl.ds(m, plan.wide)].reshape(plan.wide * slots, d_model)).astype(BF16)
            for k in range(1, GROUP):
                out_copy(c, k).wait_send()
            send[c] = packed.reshape(GROUP, Z, d_model)
            for k in range(GROUP - 1, 0, -1):
                back_copy(c, k).start()
            rrecv[c, 0] = send[c, 0]

    def combine(c, count, fresh):
        want = trow[:, 0:count * ROWS] + float(c * Z)
        for m in range(count):
            for k in range(1, GROUP):
                back_copy(c + m, k).wait_recv()

        @pl.loop(0, n_tok // TTILE)
        def _(t):
            at = pl.ds(pl.multiple_of(t * TTILE, TTILE), TTILE)
            rows = rrecv[c:c + count].reshape(count * ROWS, d_model)
            new = dot(hot(qcol[at, 0:1] == want), rows).astype(BF16)
            got[at, :] = new if fresh else got[at, :] + new

    c = 0
    for count in plan.batches:
        combine(c, count, c == 0)
        c += count

    for k in range(1, GROUP):
        count_copy(k).wait_send()

    @pl.loop(0, nc)
    def _(c):
        for k in range(1, GROUP):
            back_copy(c, k).wait_send()


def solution(mesh):
    dev_axes = ('ep2', 'ep')

    def local_step(x_loc, ids_loc, gate_loc, w_a, w_b):
        n_tok, d_model = x_loc.shape
        capacity = 8 * ((5 * GROUP * n_tok) // (32 * EXPERTS))
        vmem = pl.BlockSpec(memory_space=pltpu.VMEM)
        hbm = pl.BlockSpec(memory_space=pl.ANY)
        dma = pltpu.SemaphoreType.DMA
        args = (ids_loc.reshape(1, n_tok), x_loc, w_a, w_b)

        def moe(plan, number):
            nc, ns = plan.chunks, plan.slots
            block = pltpu.VMEM((nc, GROUP, Z, d_model), BF16)
            return pl.pallas_call(
                functools.partial(moe_kernel, plan, capacity),
                out_shape=(jax.ShapeDtypeStruct((n_tok, d_model), BF16), jax.ShapeDtypeStruct((1, 1), F32)),
                in_specs=[vmem] + [hbm] * 3, out_specs=(vmem, pl.BlockSpec(memory_space=pltpu.SMEM)),
                scratch_shapes=[
                    pltpu.VMEM((n_tok, d_model), BF16), block, block, block,
                    pltpu.VMEM((PER * capacity, d_model), BF16), pltpu.VMEM((SETS, PER * capacity, d_model), BF16),
                    pltpu.VMEM((PER * capacity, d_model), F32),
                    pltpu.VMEM((ns, d_model, FTILE), BF16), pltpu.VMEM((ns, FTILE, d_model), BF16),
                    pltpu.VMEM((GROUP, E_LOC + 8, 128), F32), pltpu.VMEM((GROUP, E_LOC + 8, 128), F32),
                    pltpu.VMEM((8, n_tok), F32), pltpu.VMEM((n_tok, 128), F32),
                    pltpu.VMEM((nc, 8, ROWS), F32), pltpu.VMEM((nc, ROWS, 128), F32),
                    dma(()), dma((GROUP,)), dma((GROUP,)),
                    dma((nc, GROUP)), dma((nc, GROUP)), dma((nc, GROUP)), dma((nc, GROUP)), dma((ns,)), dma((ns,)),
                ],
                compiler_params=pltpu.CompilerParams(
                    collective_id=number, has_side_effects=True, vmem_limit_bytes=66_000_000),
                name='moe_' + str(nc),
            )(*args)

        got, flag = moe(FAST, 0)
        got = lax.cond(flag[0, 0] > 0.0, lambda: moe(SAFE, 1)[0], lambda: got)
        return (x_loc.astype(F32) + gate_loc * got.astype(F32)).astype(BF16)

    tok_spec = P(('dp', 'ep2', 'ep'), None)
    w_spec = P(dev_axes, None, None)
    return jax.shard_map(local_step, mesh=mesh, in_specs=(tok_spec, tok_spec, tok_spec, w_spec, w_spec), out_specs=tok_spec, check_vma=False)
```

profile of v0, /device:TPU:0, one launch (start us, length us, event | category | flops | bytes accessed | tf_op | source)
XLA Modules:
  0.0 115.7 jit_solution(165372340224820891)
XLA Ops:
  0.0 0.0 copy-start
  0.0 108.8 %moe_11.1 = (bf16[2048,768]{1,0:T(8,128)(2,1)}, f32[1,1]{1,0:T(1,128)}) custom-call(s32[1,2048]{1,0:T(1,128)} %bitcast.3, bf16[2048,768]{1,0:T(8,128)(2,1)} %x_hbm.1, bf16[16,768,3072]{2,1,0:T(8,128)(2,1)} %w_in.1, bf16[16,3072,768]{2,1,0:T(8,128)(2,1)} %w_out.1), custom_call_target="tpu_custom_call" | custom-call | tf_op jit(solution)/shard_map/moe_11/pallas_call | solution.py:303
  109.5 0.0 copy-done
  109.5 0.0 copy-start.1
  109.6 0.2 conditional.1
  109.8 0.5 copy-done.1
  110.2 5.5 %add_convert_fusion = bf16[2048,768]{1,0:T(8,128)(2,1)} fusion(bf16[2048,768]{1,0:T(8,128)(2,1)} %get-tuple-element.32, bf16[2048,768]{1,0:T(8,128)(2,1)} %x_hbm.1, f32[2048]{0:T(1024)S(1)} %bitcast.5), kind=kLoop, calls=%fused_computation | loop fusion | flops 7864320 | bytes 9445376 | tf_op jit(solution)/shard_map/convert_element_type | solution.py:325
Async XLA Ops:
  0.0 109.5 %copy-start = (s32[2048,1]{0,1:T(1,128)S(1)}, s32[2048,1]{0,1:T(1,128)}, u32[]{:S(2)}) copy-start(s32[2048,1]{0,1:T(1,128)} %param.8) | copy-start | bytes 24580
  109.5 0.7 copy-start.1
where the time goes:
time: 116 us
  Pallas kernels  109 us (94%)
  other arithmetic  5.49 us (5%)
    pallas_call x1, Pallas kernels, moe(): pl.pallas_call(functools.partial(moe_kernel, plan, capacity), out_shape=(...  109 us
    convert_element_type x1, other arithmetic, local_step(): return (x_loc.astype(F32) + gate_loc * got.astype(F32)).astype(BF16)  5.49 us

commit v1 on v0

--- a/solution.py
+++ b/solution.py
@@ -20,6 +20,8 @@
 SETS = E_LOC // PER
 FTILE = 1536
 TTILE = 256
+XTILE = 512
+CTILE = 1024
 
 
 def pick(values, i):
@@ -34,7 +36,7 @@
         self.lo, self.hi, self.slots = lo, hi, slots
         self.chunks = hi[-1]
         self.batches = batches
-        assert sum(batches) == self.chunks
+        assert sum(batches) in (self.chunks, self.chunks - 1)
         self.hi_before = (0,) + hi[:-1]
         self.lo_next = lo[1:] + (self.chunks,)
         self.pairs = tuple((h - l + 1) // 2 for l, h in zip(lo, hi))
@@ -45,7 +47,7 @@
         assert all(h >= 2 * p for h, p in zip(hi, self.pairs))
 
 
-FAST = Plan((0, 1, 2, 3, 4, 6, 7, 9), (2, 4, 6, 7, 8, 9, 10, 11), 5, (4, 4, 2, 1))
+FAST = Plan((0, 0, 2, 3, 4, 6, 7, 9), (2, 4, 6, 7, 8, 9, 11, 11), 5, (4, 4, 2))
 SAFE = Plan((0,) * 8, (2, 4, 6, 8, 10, 12, 14, 16), 3, (4, 4, 4, 4))
 
 
@@ -74,9 +76,9 @@
     return jnp.dot(a, b, preferred_element_type=F32)
 
 
-def moe_kernel(plan, capacity, ids_ref, x_hbm, w_in, w_out, got, flag_ref,
-               xv, send, recv, rrecv, bbuf, obuf, acc, wi, wo, xbuf, cbuf, qrow, qcol, dlc, drc,
-               x_sem, n_send, n_recv, s_send, s_recv, r_send, r_recv, wi_sem, wo_sem):
+def moe_kernel(plan, capacity, ids_ref, gate_ref, x_hbm, w_in, w_out, y_hbm, tail_ref, cols_hbm, flag_ref,
+               xv, got, send, recv, rrecv, bbuf, obuf, acc, wi, wo, xbuf, cbuf, qrow, qcol, dlc, drc,
+               x_sem, y_sem, c_sem, n_send, n_recv, s_send, s_recv, r_send, r_recv, wi_sem, wo_sem):
     nc, ns = plan.chunks, plan.slots
     n_tok, d_model = xv.shape
     per_e = w_in.shape[2] // FTILE
@@ -90,6 +92,14 @@
         return (pltpu.make_async_copy(w_in.at[e, :, cols], wi.at[slot], wi_sem.at[slot]),
                 pltpu.make_async_copy(w_out.at[e, cols, :], wo.at[slot], wo_sem.at[slot]))
 
+    def x_copy(q):
+        at = pl.ds(q * XTILE, XTILE)
+        return pltpu.make_async_copy(x_hbm.at[at, :], xv.at[at, :], x_sem.at[q])
+
+    def y_copy(t):
+        at = pl.ds(pl.multiple_of(t * TTILE, TTILE), TTILE)
+        return pltpu.make_async_copy(got.at[at, :], y_hbm.at[at, :], y_sem.at[t])
+
     def remote(src, dst, sent, received, k):
         return pltpu.make_async_remote_copy(src_ref=src, dst_ref=dst, send_sem=sent, recv_sem=received,
                                             device_id=partner(where, k)[1], device_id_type=MESH)
@@ -106,8 +116,8 @@
     barrier = pltpu.get_barrier_semaphore()
     for k in range(1, GROUP):
         pl.semaphore_signal(barrier, inc=1, device_id=partner(where, k)[1], device_id_type=MESH)
-    x_copy = pltpu.make_async_copy(x_hbm, xv, x_sem)
-    x_copy.start()
+    for q in range(n_tok // XTILE):
+        x_copy(q).start()
 
     obuf[...] = jnp.zeros_like(obuf)
 
@@ -170,22 +180,35 @@
     pl.semaphore_wait(barrier, GROUP - 1)
     for k in range(1, GROUP):
         count_copy(k).start()
-    x_copy.wait()
+    def send_out(c):
+        for k in range(GROUP - 1, 0, -1):
+            out_copy(c, k).start()
+        recv[c, 0] = send[c, 0]
+
+    packed = jnp.zeros((ROWS, d_model), F32)
+    for q in range(n_tok // XTILE):
+        x_copy(q).wait()
+        at = slice(q * XTILE, (q + 1) * XTILE)
+        packed = packed + dot(hot(tcol == qrow[0:1, at]), xv[at, :])
+    send[0] = packed.astype(BF16).reshape(GROUP, Z, d_model)
+    send_out(0)
+
     for i in range(ns):
         for copy in w_copies(i, i):
             copy.start()
 
-    @pl.loop(0, nc)
+    @pl.loop(1, nc)
     def _(c):
         mask = (tcol + (c * Z).astype(F32)) == qrow[0:1, :]
         send[c] = dot(hot(mask), xv[...]).astype(BF16).reshape(GROUP, Z, d_model)
-        for k in range(GROUP - 1, 0, -1):
-            out_copy(c, k).start()
-        recv[c, 0] = send[c, 0]
+        send_out(c)
 
     for b in range(n_tok // TTILE):
-        piece = jnp.broadcast_to(qrow[0:1, b * TTILE:(b + 1) * TTILE], (128, TTILE))
-        qcol[b * TTILE:(b + 1) * TTILE, :] = jnp.transpose(piece)
+        at = slice(b * TTILE, (b + 1) * TTILE)
+        both = jnp.where(iota((128, TTILE), 0) == 0, qrow[0:1, at], gate_ref[0:1, at])
+        qcol[at, :] = jnp.transpose(both)
+    c_copy = pltpu.make_async_copy(qcol, cols_hbm, c_sem)
+    c_copy.start()
     for k in range(1, GROUP):
         count_copy(k).wait_recv()
     flag_ref[0, 0] = jnp.max(cbuf[:, E_LOC:E_LOC + 8, :])
@@ -259,7 +282,7 @@
                 back_copy(c, k).start()
             rrecv[c, 0] = send[c, 0]
 
-    def combine(c, count, fresh):
+    def combine(c, count, fresh, finish):
         want = trow[:, 0:count * ROWS] + float(c * Z)
         for m in range(count):
             for k in range(1, GROUP):
@@ -269,13 +292,24 @@
         def _(t):
             at = pl.ds(pl.multiple_of(t * TTILE, TTILE), TTILE)
             rows = rrecv[c:c + count].reshape(count * ROWS, d_model)
-            new = dot(hot(qcol[at, 0:1] == want), rows).astype(BF16)
-            got[at, :] = new if fresh else got[at, :] + new
+            new = dot(hot(qcol[at, 0:1] == want), rows)
+            if not fresh:
+                new = got[at, :].astype(F32) + new
+            if finish:
+                new = xv[at, :].astype(F32) + qcol[at, 1:2] * new
+            got[at, :] = new.astype(BF16)
+            if finish:
+                y_copy(t).start()
 
     c = 0
     for count in plan.batches:
-        combine(c, count, c == 0)
+        combine(c, count, c == 0, c + count == sum(plan.batches))
         c += count
+
+    if c < nc:
+        for k in range(1, GROUP):
+            back_copy(c, k).wait_recv()
+    tail_ref[...] = rrecv[nc - 1]
 
     for k in range(1, GROUP):
         count_copy(k).wait_send()
@@ -284,6 +318,17 @@
     def _(c):
         for k in range(1, GROUP):
             back_copy(c, k).wait_send()
+
+    c_copy.wait()
+    for t in range(n_tok // TTILE):
+        y_copy(t).wait()
+
+
+def close_kernel(shift, y1_ref, tail_ref, cols_ref, y_ref):
+    i = iota((1, ROWS), 1)
+    want = ((i // Z) * (SPAN - Z) + i + shift).astype(F32)
+    new = dot(hot(cols_ref[:, 0:1] == want), tail_ref[...])
+    y_ref[...] = (y1_ref[...].astype(F32) + cols_ref[:, 1:2] * new).astype(BF16)
 
 
 def solution(mesh):
@@ -295,24 +340,27 @@
         vmem = pl.BlockSpec(memory_space=pltpu.VMEM)
         hbm = pl.BlockSpec(memory_space=pl.ANY)
         dma = pltpu.SemaphoreType.DMA
-        args = (ids_loc.reshape(1, n_tok), x_loc, w_a, w_b)
+        gate_row = gate_loc.reshape(1, n_tok)
+        args = (ids_loc.reshape(1, n_tok), gate_row, x_loc, w_a, w_b)
 
         def moe(plan, number):
             nc, ns = plan.chunks, plan.slots
             block = pltpu.VMEM((nc, GROUP, Z, d_model), BF16)
             return pl.pallas_call(
                 functools.partial(moe_kernel, plan, capacity),
-                out_shape=(jax.ShapeDtypeStruct((n_tok, d_model), BF16), jax.ShapeDtypeStruct((1, 1), F32)),
-                in_specs=[vmem] + [hbm] * 3, out_specs=(vmem, pl.BlockSpec(memory_space=pltpu.SMEM)),
+                out_shape=(jax.ShapeDtypeStruct((n_tok, d_model), BF16), jax.ShapeDtypeStruct((GROUP, Z, d_model), BF16),
+                           jax.ShapeDtypeStruct((n_tok, 128), F32), jax.ShapeDtypeStruct((1, 1), F32)),
+                in_specs=[vmem] * 2 + [hbm] * 3, out_specs=(hbm, vmem, hbm, pl.BlockSpec(memory_space=pltpu.SMEM)),
                 scratch_shapes=[
-                    pltpu.VMEM((n_tok, d_model), BF16), block, block, block,
+                    pltpu.VMEM((n_tok, d_model), BF16), pltpu.VMEM((n_tok, d_model), BF16),
+                    block, block, block,
                     pltpu.VMEM((PER * capacity, d_model), BF16), pltpu.VMEM((SETS, PER * capacity, d_model), BF16),
                     pltpu.VMEM((PER * capacity, d_model), F32),
                     pltpu.VMEM((ns, d_model, FTILE), BF16), pltpu.VMEM((ns, FTILE, d_model), BF16),
                     pltpu.VMEM((GROUP, E_LOC + 8, 128), F32), pltpu.VMEM((GROUP, E_LOC + 8, 128), F32),
                     pltpu.VMEM((8, n_tok), F32), pltpu.VMEM((n_tok, 128), F32),
                     pltpu.VMEM((nc, 8, ROWS), F32), pltpu.VMEM((nc, ROWS, 128), F32),
-                    dma(()), dma((GROUP,)), dma((GROUP,)),
+                    dma((n_tok // XTILE,)), dma((n_tok // TTILE,)), dma(()), dma((GROUP,)), dma((GROUP,)),
                     dma((nc, GROUP)), dma((nc, GROUP)), dma((nc, GROUP)), dma((nc, GROUP)), dma((ns,)), dma((ns,)),
                 ],
                 compiler_params=pltpu.CompilerParams(
@@ -320,9 +368,15 @@
                 name='moe_' + str(nc),
             )(*args)
 
-        got, flag = moe(FAST, 0)
-        got = lax.cond(flag[0, 0] > 0.0, lambda: moe(SAFE, 1)[0], lambda: got)
-        return (x_loc.astype(F32) + gate_loc * got.astype(F32)).astype(BF16)
+        y1, tail, cols, flag = moe(FAST, 0)
+        y1, tail = lax.cond(flag[0, 0] > 0.0, lambda: (moe(SAFE, 1)[0], jnp.zeros_like(tail)), lambda: (y1, tail))
+        rows = lambda width: pl.BlockSpec((CTILE, width), lambda t: (t, 0))
+        return pl.pallas_call(
+            functools.partial(close_kernel, (FAST.chunks - 1) * Z),
+            out_shape=jax.ShapeDtypeStruct((n_tok, d_model), BF16), grid=(n_tok // CTILE,),
+            in_specs=[rows(d_model), pl.BlockSpec((ROWS, d_model), lambda t: (0, 0)), rows(128)], out_specs=rows(d_model),
+            name='close',
+        )(y1, tail.reshape(ROWS, d_model), cols)
 
     tok_spec = P(('dp', 'ep2', 'ep'), None)
     w_spec = P(dev_axes, None, None)

time: 116 us -> 111 us (0.957)
  other arithmetic: 5.49 us -> 0 us
    convert_element_type x1 -> x0, other arithmetic: 5.49 us -> none  [local_step(): return (x_loc.astype(F32) + gate_loc * got.astype(F32)).astype(BF16)]
    pallas_call x0 -> x1, Pallas kernels: none -> 4.06 us  [local_step(): pl.pallas_call(functools.partial(close_kernel, (FAST.chunks - 1) * Z), ou...]
    pallas_call x1, Pallas kernels: 109 us -> 106 us  [moe(): pl.pallas_call(functools.partial(moe_kernel, plan, capacity), out_shape=(...]
where the time goes in v1:
time: 111 us
  Pallas kernels  110 us (99%)
    pallas_call x1, Pallas kernels, moe(): pl.pallas_call(functools.partial(moe_kernel, plan, capacity), out_shape=(...  106 us
    pallas_call x1, Pallas kernels, local_step(): pl.pallas_call(functools.partial(close_kernel, (FAST.chunks - 1) * Z), ou...  4.06 us

profile of v1, /device:TPU:0, one launch (start us, length us, event | category | flops | bytes accessed | tf_op | source)
XLA Modules:
  0.0 110.8 jit_solution(7267857656966514493)
XLA Ops:
  0.0 0.0 copy-start
  0.0 0.0 copy-start.1
  0.0 105.9 %moe_11.1 = (bf16[2048,768]{1,0:T(8,128)(2,1)}, bf16[8,32,768]{2,1,0:T(8,128)(2,1)S(1)}, f32[2048,128]{1,0:T(8,128)}, f32[1,1]{1,0:T(1,128)}) custom-call(s32[1,2048]{1,0:T(1,128)} %bitcast.5, f32[1,2048]{1,0:T(1,128)} %bitcast.7, bf16[2048,768]{1,0:T(8,128)(2,1)} %x_hbm.1, bf16[16,768,3072]{2,1,0:T(8,128)(2,1)} %w_in.1, bf16[16,3072,768]{2,1,0:T(8,128)(2,1)} %w_out.1), custom_call_target="tpu_custom_call" | custom-call | tf_op jit(solution)/shard_map/moe_11/pallas_call | solution.py:349
  106.5 0.0 copy-done
  106.5 0.0 copy-done.1
  106.5 0.2 conditional.1
  106.7 4.1 %close.1 = bf16[2048,768]{1,0:T(8,128)(2,1)} custom-call(bf16[2048,768]{1,0:T(8,128)(2,1)} %get-tuple-element.39.y1_ref, bf16[256,768]{1,0:T(8,128)(2,1)S(1)} %get-tuple-element.40.tail_ref, f32[2048,128]{1,0:T(8,128)} %get-tuple-element.41.cols_ref), custom_call_target="tpu_custom_call" | custom-call | tf_op jit(solution)/shard_map/close/pallas_call | solution.py:374
Async XLA Ops:
  0.0 106.5 %copy-start = (s32[2048,1]{0,1:T(1,128)S(1)}, s32[2048,1]{0,1:T(1,128)}, u32[]{:S(2)}) copy-start(s32[2048,1]{0,1:T(1,128)} %param.8) | copy-start | bytes 24580
  0.0 106.5 %copy-start.1 = (f32[2048,1]{0,1:T(1,128)S(1)}, f32[2048,1]{0,1:T(1,128)}, u32[]{:S(2)}) copy-start(f32[2048,1]{0,1:T(1,128)} %param.9) | copy-start | bytes 24580

commit v2 on v1

--- a/solution.py
+++ b/solution.py
@@ -32,23 +32,25 @@
 
 
 class Plan:
-    def __init__(self, lo, hi, slots, batches):
-        self.lo, self.hi, self.slots = lo, hi, slots
-        self.chunks = hi[-1]
+    def __init__(self, lo, hi, slots, batches, shared):
+        self.lo, self.hi, self.slots, self.shared = lo, hi, slots, shared
+        self.places = hi[-1]
+        self.chunks = self.places - shared
         self.batches = batches
         assert sum(batches) in (self.chunks, self.chunks - 1)
         self.hi_before = (0,) + hi[:-1]
-        self.lo_next = lo[1:] + (self.chunks,)
+        self.lo_next = lo[1:] + (self.chunks - shared,)
+        assert all(a <= b for a, b in zip(lo, self.lo_next))
         self.pairs = tuple((h - l + 1) // 2 for l, h in zip(lo, hi))
-        first = [min(m for m in range(SETS) if hi[m] > c) for c in range(self.chunks)]
-        after = [max(m for m in range(SETS) if lo[m] <= c) + 1 for c in range(self.chunks)]
+        first = [min(m for m in range(SETS) if hi[m] > c) for c in range(self.places)]
+        after = [max(m for m in range(SETS) if lo[m] <= c) + 1 for c in range(self.places)]
         self.wide = max(b - a for a, b in zip(first, after))
         self.first = tuple(min(m, SETS - self.wide) for m in first)
         assert all(h >= 2 * p for h, p in zip(hi, self.pairs))
 
 
-FAST = Plan((0, 0, 2, 3, 4, 6, 7, 9), (2, 4, 6, 7, 8, 9, 11, 11), 5, (4, 4, 2))
-SAFE = Plan((0,) * 8, (2, 4, 6, 8, 10, 12, 14, 16), 3, (4, 4, 4, 4))
+FAST = Plan((0, 0, 1, 2, 3, 5, 6, 7), (2, 4, 6, 7, 8, 9, 10, 11), 5, (4, 4, 1), 1)
+SAFE = Plan((0,) * 8, (2, 4, 6, 8, 10, 12, 14, 16), 3, (4, 4, 4, 4), 0)
 
 
 def position():
@@ -77,8 +79,8 @@
 
 
 def moe_kernel(plan, capacity, ids_ref, gate_ref, x_hbm, w_in, w_out, y_hbm, tail_ref, cols_hbm, flag_ref,
-               xv, got, send, recv, rrecv, bbuf, obuf, acc, wi, wo, xbuf, cbuf, qrow, qcol, dlc, drc,
-               x_sem, y_sem, c_sem, n_send, n_recv, s_send, s_recv, r_send, r_recv, wi_sem, wo_sem):
+               xv, got, send, recv, rrecv, xsend, xrecv, bbuf, obuf, acc, wi, wo, xbuf, cbuf, qrow, qcol, dlc, drc,
+               x_sem, y_sem, c_sem, n_send, n_recv, s_send, s_recv, r_send, r_recv, x_send, x_recv, wi_sem, wo_sem):
     nc, ns = plan.chunks, plan.slots
     n_tok, d_model = xv.shape
     per_e = w_in.shape[2] // FTILE
@@ -109,6 +111,12 @@
 
     def out_copy(c, k):
         return remote(send.at[c, k], recv.at[c, k], s_send.at[c, k], s_recv.at[c, k], k)
+
+    def pass_on():
+        return remote(recv.at[nc - 1], recv.at[nc], x_send.at[0], x_recv.at[0], 1)
+
+    def hand_over():
+        return remote(xsend, xrecv, x_send.at[1], x_recv.at[1], 1)
 
     def back_copy(c, k):
         return remote(send.at[c, k], rrecv.at[c, k], r_send.at[c, k], r_recv.at[c, k], k)
@@ -137,6 +145,9 @@
             mine = jnp.where(in_row == g, base, mine)
             base = base + dot(sums[g], counts)
             over = jnp.maximum(over, base - float(plan.hi[g] * Z))
+        if plan.shared:
+            other = jnp.concatenate([base[(b ^ 1) * E_LOC:((b ^ 1) + 1) * E_LOC] for b in range(GROUP)], axis=0)
+            over = jnp.maximum(over, base + other - float(2 * nc * Z))
         return mine + dot(inner, counts), over
 
     chosen = hot(iota((EXPERTS, n_tok), 0) == ids_ref[...])
@@ -152,6 +163,11 @@
         rank = dot(part, upper)
         full = jnp.concatenate([rank[:, i * 128:(i + 1) * 128] + base for i in range(TTILE // 128)], axis=1)
         code = jnp.sum(part.astype(F32) * full, axis=0, keepdims=True)
+        if plan.shared:
+            whole = code.astype(jnp.int32)
+            k, place = whole // SPAN, whole % SPAN
+            mirrored = jnp.bitwise_xor(k, 1) * SPAN + (2 * nc * Z - 1) - place
+            code = jnp.where(place >= nc * Z, mirrored, whole).astype(F32)
         qrow[:, b * TTILE:(b + 1) * TTILE] = jnp.broadcast_to(code, (8, TTILE))
         base = base + rank[:, TTILE:]
 
@@ -221,21 +237,49 @@
     last = first + kept
     shift = ((row % E_LOC) * capacity + 1).astype(F32) + ahead - first
     first, last, shift = first[:, 0:1], last[:, 0:1], shift[:, 0:1]
-    for c in range(nc):
-        at = trow[:, 0:ROWS] + float(c * Z)
+    lane = iota((1, ROWS), 1)
+    for c in range(plan.places):
+        if c < nc:
+            at = trow[:, 0:ROWS] + float(c * Z)
+        else:
+            at = (jnp.bitwise_xor(lane // Z, 1) * SPAN + (2 * nc * Z - 1 - (nc - 1) * Z) - lane % Z).astype(F32)
         slot = jnp.sum(jnp.where((at >= first) & (at < last), at + shift, 0.0), axis=0, keepdims=True) - 1.0
         dlc[c] = jnp.broadcast_to(slot, (8, ROWS))
         drc[c] = jnp.transpose(jnp.broadcast_to(slot, (128, ROWS)))
 
     slot_col = iota((slots, 1), 0).astype(F32)
     slot_row = iota((1, plan.wide * slots), 1).astype(F32)
+
+    def pack(c, m):
+        mask = drc[c, :, 0:1] == (slot_row + m * float(slots) if isinstance(m, int) else slot_row + (m * slots).astype(F32))
+        packed = dot(hot(mask), obuf[pl.ds(m, plan.wide)].reshape(plan.wide * slots, d_model))
+        return packed.astype(BF16).reshape(GROUP, Z, d_model)
+
+    def send_back(c, packed):
+        for k in range(1, GROUP):
+            out_copy(c, k).wait_send()
+        send[c] = packed
+        for k in range(GROUP - 1, 0, -1):
+            back_copy(c, k).start()
+        rrecv[c, 0] = send[c, 0]
 
     @pl.loop(0, SETS)
     def _(g):
         @pl.loop(pick(plan.hi_before, g), pick(plan.hi, g))
         def _(c):
-            for k in range(1, GROUP):
-                out_copy(c, k).wait_recv()
+            @pl.when(c < nc)
+            def _():
+                for k in range(1, GROUP):
+                    out_copy(c, k).wait_recv()
+
+            if plan.shared:
+                @pl.when(c == nc - 1)
+                def _():
+                    pass_on().start()
+
+                @pl.when(c == nc)
+                def _():
+                    pass_on().wait_recv()
 
         acc[...] = jnp.zeros_like(acc)
 
@@ -272,15 +316,14 @@
 
         @pl.loop(pick(plan.lo, g), pick(plan.lo_next, g))
         def _(c):
-            m = pick(plan.first, c)
-            mask = drc[c, :, 0:1] == (slot_row + (m * slots).astype(F32))
-            packed = dot(hot(mask), obuf[pl.ds(m, plan.wide)].reshape(plan.wide * slots, d_model)).astype(BF16)
-            for k in range(1, GROUP):
-                out_copy(c, k).wait_send()
-            send[c] = packed.reshape(GROUP, Z, d_model)
-            for k in range(GROUP - 1, 0, -1):
-                back_copy(c, k).start()
-            rrecv[c, 0] = send[c, 0]
+            send_back(c, pack(c, pick(plan.first, c)))
+
+    if plan.shared:
+        xsend[...] = pack(nc, plan.first[nc])
+        hand_over().start()
+        packed = pack(nc - 1, plan.first[nc - 1])
+        hand_over().wait_recv()
+        send_back(nc - 1, packed + xrecv[...])
 
     def combine(c, count, fresh, finish):
         want = trow[:, 0:count * ROWS] + float(c * Z)
@@ -313,6 +356,9 @@
 
     for k in range(1, GROUP):
         count_copy(k).wait_send()
+    if plan.shared:
+        pass_on().wait_send()
+        hand_over().wait_send()
 
     @pl.loop(0, nc)
     def _(c):
@@ -346,6 +392,7 @@
         def moe(plan, number):
             nc, ns = plan.chunks, plan.slots
             block = pltpu.VMEM((nc, GROUP, Z, d_model), BF16)
+            chunk = pltpu.VMEM((GROUP, Z, d_model), BF16)
             return pl.pallas_call(
                 functools.partial(moe_kernel, plan, capacity),
                 out_shape=(jax.ShapeDtypeStruct((n_tok, d_model), BF16), jax.ShapeDtypeStruct((GROUP, Z, d_model), BF16),
@@ -353,15 +400,15 @@
                 in_specs=[vmem] * 2 + [hbm] * 3, out_specs=(hbm, vmem, hbm, pl.BlockSpec(memory_space=pltpu.SMEM)),
                 scratch_shapes=[
                     pltpu.VMEM((n_tok, d_model), BF16), pltpu.VMEM((n_tok, d_model), BF16),
-                    block, block, block,
+                    block, pltpu.VMEM((plan.places, GROUP, Z, d_model), BF16), block, chunk, chunk,
                     pltpu.VMEM((PER * capacity, d_model), BF16), pltpu.VMEM((SETS, PER * capacity, d_model), BF16),
                     pltpu.VMEM((PER * capacity, d_model), F32),
                     pltpu.VMEM((ns, d_model, FTILE), BF16), pltpu.VMEM((ns, FTILE, d_model), BF16),
                     pltpu.VMEM((GROUP, E_LOC + 8, 128), F32), pltpu.VMEM((GROUP, E_LOC + 8, 128), F32),
                     pltpu.VMEM((8, n_tok), F32), pltpu.VMEM((n_tok, 128), F32),
-                    pltpu.VMEM((nc, 8, ROWS), F32), pltpu.VMEM((nc, ROWS, 128), F32),
+                    pltpu.VMEM((plan.places, 8, ROWS), F32), pltpu.VMEM((plan.places, ROWS, 128), F32),
                     dma((n_tok // XTILE,)), dma((n_tok // TTILE,)), dma(()), dma((GROUP,)), dma((GROUP,)),
-                    dma((nc, GROUP)), dma((nc, GROUP)), dma((nc, GROUP)), dma((nc, GROUP)), dma((ns,)), dma((ns,)),
+                    dma((nc, GROUP)), dma((nc, GROUP)), dma((nc, GROUP)), dma((nc, GROUP)), dma((2,)), dma((2,)), dma((ns,)), dma((ns,)),
                 ],
                 compiler_params=pltpu.CompilerParams(
                     collective_id=number, has_side_effects=True, vmem_limit_bytes=66_000_000),

time: 111 us -> 103 us (0.928)
  Pallas kernels: 110 us -> 102 us
    pallas_call x1, Pallas kernels: 106 us -> 98.1 us  [moe(): pl.pallas_call(functools.partial(moe_kernel, plan, capacity), out_shape=(...]
where the time goes in v2:
time: 103 us
  Pallas kernels  102 us (99%)
    pallas_call x1, Pallas kernels, moe(): pl.pallas_call(functools.partial(moe_kernel, plan, capacity), out_shape=(...  98.1 us
    pallas_call x1, Pallas kernels, local_step(): pl.pallas_call(functools.partial(close_kernel, (FAST.chunks - 1) * Z), ou...  4.06 us

profile of v2, /device:TPU:0, one launch (start us, length us, event | category | flops | bytes accessed | tf_op | source)
XLA Modules:
  0.0 103.0 jit_solution(17127718685882826000)
XLA Ops:
  0.0 0.0 copy-start
  0.0 0.0 copy-start.1
  0.0 98.1 %moe_10.1 = (bf16[2048,768]{1,0:T(8,128)(2,1)}, bf16[8,32,768]{2,1,0:T(8,128)(2,1)S(1)}, f32[2048,128]{1,0:T(8,128)}, f32[1,1]{1,0:T(1,128)}) custom-call(s32[1,2048]{1,0:T(1,128)} %bitcast.5, f32[1,2048]{1,0:T(1,128)} %bitcast.7, bf16[2048,768]{1,0:T(8,128)(2,1)} %x_hbm.1, bf16[16,768,3072]{2,1,0:T(8,128)(2,1)} %w_in.1, bf16[16,3072,768]{2,1,0:T(8,128)(2,1)} %w_out.1), custom_call_target="tpu_custom_call" | custom-call | tf_op jit(solution)/shard_map/moe_10/pallas_call | solution.py:396
  98.8 0.0 copy-done
  98.8 0.0 copy-done.1
  98.8 0.2 conditional.1
  99.0 4.1 %close.1 = bf16[2048,768]{1,0:T(8,128)(2,1)} custom-call(bf16[2048,768]{1,0:T(8,128)(2,1)} %get-tuple-element.39.y1_ref, bf16[256,768]{1,0:T(8,128)(2,1)S(1)} %get-tuple-element.40.tail_ref, f32[2048,128]{1,0:T(8,128)} %get-tuple-element.41.cols_ref), custom_call_target="tpu_custom_call" | custom-call | tf_op jit(solution)/shard_map/close/pallas_call | solution.py:421
Async XLA Ops:
  0.0 98.8 %copy-start = (s32[2048,1]{0,1:T(1,128)S(1)}, s32[2048,1]{0,1:T(1,128)}, u32[]{:S(2)}) copy-start(s32[2048,1]{0,1:T(1,128)} %param.8) | copy-start | bytes 24580
  0.0 98.8 %copy-start.1 = (f32[2048,1]{0,1:T(1,128)S(1)}, f32[2048,1]{0,1:T(1,128)}, u32[]{:S(2)}) copy-start(f32[2048,1]{0,1:T(1,128)} %param.9) | copy-start | bytes 24580

commit v3 on v2

--- a/solution.py
+++ b/solution.py
@@ -20,7 +20,7 @@
 SETS = E_LOC // PER
 FTILE = 1536
 TTILE = 256
-XTILE = 512
+XTILE = 2048
 CTILE = 1024
 
 
@@ -78,9 +78,9 @@
     return jnp.dot(a, b, preferred_element_type=F32)
 
 
-def moe_kernel(plan, capacity, ids_ref, gate_ref, x_hbm, w_in, w_out, y_hbm, tail_ref, cols_hbm, flag_ref,
-               xv, got, send, recv, rrecv, xsend, xrecv, bbuf, obuf, acc, wi, wo, xbuf, cbuf, qrow, qcol, dlc, drc,
-               x_sem, y_sem, c_sem, n_send, n_recv, s_send, s_recv, r_send, r_recv, x_send, x_recv, wi_sem, wo_sem):
+def moe_kernel(plan, capacity, ids_hbm, gate_hbm, x_hbm, w_in, w_out, y_hbm, tail_ref, cols_hbm, flag_hbm,
+               ids_ref, gate_ref, flag_ref, xv, got, send, recv, rrecv, xsend, xrecv, bbuf, obuf, acc, wi, wo, xbuf, cbuf, qrow, qcol, dlc, drc,
+               i_sem, x_sem, y_sem, c_sem, n_send, n_recv, s_send, s_recv, r_send, r_recv, x_send, x_recv, wi_sem, wo_sem):
     nc, ns = plan.chunks, plan.slots
     n_tok, d_model = xv.shape
     per_e = w_in.shape[2] // FTILE
@@ -121,6 +121,11 @@
     def back_copy(c, k):
         return remote(send.at[c, k], rrecv.at[c, k], r_send.at[c, k], r_recv.at[c, k], k)
 
+    ids_copy = pltpu.make_async_copy(ids_hbm, ids_ref, i_sem.at[0])
+    gate_copy = pltpu.make_async_copy(gate_hbm, gate_ref, i_sem.at[1])
+    flag_copy = pltpu.make_async_copy(flag_ref, flag_hbm, i_sem.at[2])
+    ids_copy.start()
+    gate_copy.start()
     barrier = pltpu.get_barrier_semaphore()
     for k in range(1, GROUP):
         pl.semaphore_signal(barrier, inc=1, device_id=partner(where, k)[1], device_id_type=MESH)
@@ -150,6 +155,7 @@
             over = jnp.maximum(over, base + other - float(2 * nc * Z))
         return mine + dot(inner, counts), over
 
+    ids_copy.wait()
     chosen = hot(iota((EXPERTS, n_tok), 0) == ids_ref[...])
     counts = dot(chosen, jnp.ones((n_tok, 128), BF16))
     start, over = starts(counts)
@@ -219,6 +225,7 @@
         send[c] = dot(hot(mask), xv[...]).astype(BF16).reshape(GROUP, Z, d_model)
         send_out(c)
 
+    gate_copy.wait()
     for b in range(n_tok // TTILE):
         at = slice(b * TTILE, (b + 1) * TTILE)
         both = jnp.where(iota((128, TTILE), 0) == 0, qrow[0:1, at], gate_ref[0:1, at])
@@ -228,6 +235,7 @@
     for k in range(1, GROUP):
         count_copy(k).wait_recv()
     flag_ref[0, 0] = jnp.max(cbuf[:, E_LOC:E_LOC + 8, :])
+    flag_copy.start()
     got_counts = cbuf[:, 0:E_LOC, :].reshape(EXPERTS, 128)
     start, _ = starts(got_counts)
     earlier = hot(((row % E_LOC) == (col % E_LOC)) & (jnp.bitwise_xor(col // E_LOC, me) < jnp.bitwise_xor(row // E_LOC, me)))
@@ -365,6 +373,7 @@
         for k in range(1, GROUP):
             back_copy(c, k).wait_send()
 
+    flag_copy.wait()
     c_copy.wait()
     for t in range(n_tok // TTILE):
         y_copy(t).wait()
@@ -397,8 +406,9 @@
                 functools.partial(moe_kernel, plan, capacity),
                 out_shape=(jax.ShapeDtypeStruct((n_tok, d_model), BF16), jax.ShapeDtypeStruct((GROUP, Z, d_model), BF16),
                            jax.ShapeDtypeStruct((n_tok, 128), F32), jax.ShapeDtypeStruct((1, 1), F32)),
-                in_specs=[vmem] * 2 + [hbm] * 3, out_specs=(hbm, vmem, hbm, pl.BlockSpec(memory_space=pltpu.SMEM)),
+                in_specs=[hbm] * 5, out_specs=(hbm, vmem, hbm, hbm),
                 scratch_shapes=[
+                    pltpu.VMEM((1, n_tok), jnp.int32), pltpu.VMEM((1, n_tok), F32), pltpu.SMEM((1, 1), F32),
                     pltpu.VMEM((n_tok, d_model), BF16), pltpu.VMEM((n_tok, d_model), BF16),
                     block, pltpu.VMEM((plan.places, GROUP, Z, d_model), BF16), block, chunk, chunk,
                     pltpu.VMEM((PER * capacity, d_model), BF16), pltpu.VMEM((SETS, PER * capacity, d_model), BF16),
@@ -407,7 +417,7 @@
                     pltpu.VMEM((GROUP, E_LOC + 8, 128), F32), pltpu.VMEM((GROUP, E_LOC + 8, 128), F32),
                     pltpu.VMEM((8, n_tok), F32), pltpu.VMEM((n_tok, 128), F32),
                     pltpu.VMEM((plan.places, 8, ROWS), F32), pltpu.VMEM((plan.places, ROWS, 128), F32),
-                    dma((n_tok // XTILE,)), dma((n_tok // TTILE,)), dma(()), dma((GROUP,)), dma((GROUP,)),
+                    dma((3,)), dma((n_tok // XTILE,)), dma((n_tok // TTILE,)), dma(()), dma((GROUP,)), dma((GROUP,)),
                     dma((nc, GROUP)), dma((nc, GROUP)), dma((nc, GROUP)), dma((nc, GROUP)), dma((2,)), dma((2,)), dma((ns,)), dma((ns,)),
                 ],
                 compiler_params=pltpu.CompilerParams(

time: 103 us -> 102 us (level)
    pallas_call x1, Pallas kernels: 98.1 us -> 96.7 us  [moe(): pl.pallas_call(functools.partial(moe_kernel, plan, capacity), out_shape=(...]
where the time goes in v3:
time: 102 us
  Pallas kernels  101 us (99%)
    pallas_call x1, Pallas kernels, moe(): pl.pallas_call(functools.partial(moe_kernel, plan, capacity), out_shape=(...  96.7 us
    pallas_call x1, Pallas kernels, local_step(): pl.pallas_call(functools.partial(close_kernel, (FAST.chunks - 1) * Z), ou...  4.06 us

profile of v3, /device:TPU:0, one launch (start us, length us, event | category | flops | bytes accessed | tf_op | source)
XLA Modules:
  0.0 101.6 jit_solution(16562826536933913323)
XLA Ops:
  0.0 0.0 copy-start
  0.0 0.0 copy-start.1
  0.0 96.7 %moe_10.1 = (bf16[2048,768]{1,0:T(8,128)(2,1)}, bf16[8,32,768]{2,1,0:T(8,128)(2,1)S(1)}, f32[2048,128]{1,0:T(8,128)}, f32[1,1]{1,0:T(1,128)}) custom-call(s32[1,2048]{1,0:T(1,128)} %bitcast.5, f32[1,2048]{1,0:T(1,128)} %bitcast.7, bf16[2048,768]{1,0:T(8,128)(2,1)} %x_hbm.1, bf16[16,768,3072]{2,1,0:T(8,128)(2,1)} %w_in.1, bf16[16,3072,768]{2,1,0:T(8,128)(2,1)} %w_out.1), custom_call_target="tpu_custom_call" | custom-call | tf_op jit(solution)/shard_map/moe_10/pallas_call | solution.py:405
  97.3 0.0 copy-done
  97.3 0.0 copy-done.1
  97.3 0.2 conditional.1
  97.5 4.1 %close.1 = bf16[2048,768]{1,0:T(8,128)(2,1)} custom-call(bf16[2048,768]{1,0:T(8,128)(2,1)} %get-tuple-element.39.y1_ref, bf16[256,768]{1,0:T(8,128)(2,1)S(1)} %get-tuple-element.40.tail_ref, f32[2048,128]{1,0:T(8,128)} %get-tuple-element.41.cols_ref), custom_call_target="tpu_custom_call" | custom-call | tf_op jit(solution)/shard_map/close/pallas_call | solution.py:431
Async XLA Ops:
  0.0 97.3 %copy-start = (s32[2048,1]{0,1:T(1,128)S(1)}, s32[2048,1]{0,1:T(1,128)}, u32[]{:S(2)}) copy-start(s32[2048,1]{0,1:T(1,128)} %param.8) | copy-start | bytes 24580
  0.0 97.3 %copy-start.1 = (f32[2048,1]{0,1:T(1,128)S(1)}, f32[2048,1]{0,1:T(1,128)}, u32[]{:S(2)}) copy-start(f32[2048,1]{0,1:T(1,128)} %param.9) | copy-start | bytes 24580

commit v4 on v3

--- a/solution.py
+++ b/solution.py
@@ -199,9 +199,6 @@
     tcol = targets((ROWS, 1), 0)
     trow = targets((1, 4 * ROWS), 1)
 
-    pl.semaphore_wait(barrier, GROUP - 1)
-    for k in range(1, GROUP):
-        count_copy(k).start()
     def send_out(c):
         for k in range(GROUP - 1, 0, -1):
             out_copy(c, k).start()
@@ -213,7 +210,10 @@
         at = slice(q * XTILE, (q + 1) * XTILE)
         packed = packed + dot(hot(tcol == qrow[0:1, at]), xv[at, :])
     send[0] = packed.astype(BF16).reshape(GROUP, Z, d_model)
+    pl.semaphore_wait(barrier, GROUP - 1)
     send_out(0)
+    for k in range(1, GROUP):
+        count_copy(k).start()
 
     for i in range(ns):
         for copy in w_copies(i, i):

time: 102 us -> 103 us (level)
    pallas_call x1, Pallas kernels: 96.7 us -> 98 us  [moe(): pl.pallas_call(functools.partial(moe_kernel, plan, capacity), out_shape=(...]
where the time goes in v4:
time: 103 us
  Pallas kernels  102 us (99%)
    pallas_call x1, Pallas kernels, moe(): pl.pallas_call(functools.partial(moe_kernel, plan, capacity), out_shape=(...  98 us
    pallas_call x1, Pallas kernels, local_step(): pl.pallas_call(functools.partial(close_kernel, (FAST.chunks - 1) * Z), ou...  4.06 us

profile of v4, /device:TPU:0, one launch (start us, length us, event | category | flops | bytes accessed | tf_op | source)
XLA Modules:
  0.0 102.9 jit_solution(11417806562920951116)
XLA Ops:
  0.0 0.0 copy-start
  0.0 0.0 copy-start.1
  0.0 98.0 %moe_10.1 = (bf16[2048,768]{1,0:T(8,128)(2,1)}, bf16[8,32,768]{2,1,0:T(8,128)(2,1)S(1)}, f32[2048,128]{1,0:T(8,128)}, f32[1,1]{1,0:T(1,128)}) custom-call(s32[1,2048]{1,0:T(1,128)} %bitcast.5, f32[1,2048]{1,0:T(1,128)} %bitcast.7, bf16[2048,768]{1,0:T(8,128)(2,1)} %x_hbm.1, bf16[16,768,3072]{2,1,0:T(8,128)(2,1)} %w_in.1, bf16[16,3072,768]{2,1,0:T(8,128)(2,1)} %w_out.1), custom_call_target="tpu_custom_call" | custom-call | tf_op jit(solution)/shard_map/moe_10/pallas_call | solution.py:405
  98.6 0.0 copy-done
  98.6 0.0 copy-done.1
  98.6 0.2 conditional.1
  98.8 4.1 %close.1 = bf16[2048,768]{1,0:T(8,128)(2,1)} custom-call(bf16[2048,768]{1,0:T(8,128)(2,1)} %get-tuple-element.39.y1_ref, bf16[256,768]{1,0:T(8,128)(2,1)S(1)} %get-tuple-element.40.tail_ref, f32[2048,128]{1,0:T(8,128)} %get-tuple-element.41.cols_ref), custom_call_target="tpu_custom_call" | custom-call | tf_op jit(solution)/shard_map/close/pallas_call | solution.py:431
Async XLA Ops:
  0.0 98.6 %copy-start = (s32[2048,1]{0,1:T(1,128)S(1)}, s32[2048,1]{0,1:T(1,128)}, u32[]{:S(2)}) copy-start(s32[2048,1]{0,1:T(1,128)} %param.8) | copy-start | bytes 24580
  0.0 98.6 %copy-start.1 = (f32[2048,1]{0,1:T(1,128)S(1)}, f32[2048,1]{0,1:T(1,128)}, u32[]{:S(2)}) copy-start(f32[2048,1]{0,1:T(1,128)} %param.9) | copy-start | bytes 24580
